TPU v7x, 512 devices: a whole 4x8x8 slice. The times are simulated.
512 devices in a mesh: space: 64 (over y_lo, z, x), tensor: 8 (over y_hi, core).
Axes of the slice: x: 4, y: 8 (y_hi: 4, y_lo: 2; y = y_hi * 2 + y_lo), z: 8, core: 2. Of those that a mesh axis runs over, the one named last changes fastest.
Arguments:
- tokens: float32 [2, 128, 128, 2048], P(None, 'space', None, 'tensor'), may hold values from -6 to 6
- in_gain: float32 [2048], replicated, may hold values from 0.25 to 1.75
- w_inner: bfloat16 [2048, 3072], P(None, 'tensor'), may hold values from -0.125 to 0.125
- w_bc: bfloat16 [2048, 256], replicated, may hold values from -0.03125 to 0.03125
- w_step: bfloat16 [2048, 48], P(None, 'tensor'), may hold values from -0.125 to 0.125
- step_bias: float32 [48], P('tensor'), may hold values from -3 to 0
- decay_rate: float32 [48], P('tensor'), may hold values from 0.02 to 2
- skip: float32 [48], P('tensor'), may hold values from 0.5 to 2
- norm_gain: float32 [3072], P('tensor'), may hold values from 0.25 to 1.75
- w_out: bfloat16 [3072, 2048], P('tensor'), may hold values from -0.109375 to 0.109375
Outputs:
- mixed: bfloat16 [2, 128, 128, 2048], P(None, 'space', None, 'tensor')
All inputs are finite; a program needn't handle non-finite values.
Results may differ from a plain program's by a relative error of at most 0.011.
Values may be sent and summed in bfloat16 or wider, within the bound.
No kernel may reach another device: no remote copies, remote signals or barrier semaphores. Data moves between devices by JAX's collectives and lax.ppermute only.
A program may use at most 64 MiB of HBM per device.

v0:
```python
import jax
import jax.numpy as jnp
from jax import lax
from jax.sharding import PartitionSpec as P

HEAD_DIM = 64
STATE = 128
NORM_HEADS = 6
EPS = 1e-05


def kernel(logdecay):
    running = jnp.cumsum(logdecay, axis=-1)
    length = logdecay.shape[-1]
    place = jnp.arange(length)
    lower = place[:, None] >= place[None, :]
    upper = place[:, None] <= place[None, :]
    later = running[..., :, None] - running[..., None, :]
    shifted = running - logdecay
    earlier = shifted[..., None, :] - shifted[..., :, None]
    forward = jnp.exp(jnp.where(lower, later, -jnp.inf))
    backward = jnp.exp(jnp.where(upper, earlier, -jnp.inf))
    return forward + backward


def scan_grid(values, maps, logdecay, along_rows):
    heads = logdecay.shape[-1]
    in_map = maps[..., :STATE]
    out_map = maps[..., STATE:]
    split_values = values.reshape(values.shape[:3] + (heads, HEAD_DIM))
    if along_rows:
        scores = jnp.einsum("ialn,iamn->ialm", out_map, in_map, preferred_element_type=jnp.float32)
        decays = jnp.moveaxis(logdecay.astype(jnp.float32), 3, 2)
    else:
        scores = jnp.einsum("ilan,iman->ialm", out_map, in_map, preferred_element_type=jnp.float32)
        decays = jnp.transpose(logdecay.astype(jnp.float32), (0, 2, 3, 1))
    weights = (scores[:, :, None] * kernel(decays)).astype(jnp.bfloat16)
    if along_rows:
        result = jnp.einsum(
            "iahlm,iamhp->ialhp", weights, split_values, preferred_element_type=jnp.float32
        )
    else:
        result = jnp.einsum(
            "iahlm,imahp->ilahp", weights, split_values, preferred_element_type=jnp.float32
        )
    return result.reshape(values.shape)


def on_device(
    tokens, in_gain, w_inner, w_bc, w_step, step_bias, decay_rate, skip, norm_gain, w_out
):
    whole = lax.all_gather(tokens.astype(jnp.bfloat16), "tensor", axis=3, tiled=True)
    rounded = whole.astype(jnp.float32)
    scale = lax.rsqrt(jnp.mean(rounded * rounded, axis=-1, keepdims=True) + EPS)
    normed = (rounded * scale * in_gain).astype(jnp.bfloat16)
    inner = jnp.einsum("irwd,dc->irwc", normed, w_inner, preferred_element_type=jnp.float32).astype(
        jnp.bfloat16
    )
    maps = jnp.einsum("irwd,dc->irwc", normed, w_bc, preferred_element_type=jnp.float32).astype(
        jnp.bfloat16
    )
    step = jax.nn.softplus(
        jnp.einsum("irwd,dc->irwc", normed, w_step, preferred_element_type=jnp.float32) + step_bias
    )
    logdecay = (-decay_rate * step).astype(jnp.bfloat16)
    heads_local = w_step.shape[1]
    lead = inner.shape[:3]
    value = (
        (inner.reshape(lead + (heads_local, HEAD_DIM)).astype(jnp.float32) * step[..., None])
        .reshape(inner.shape)
        .astype(jnp.bfloat16)
    )
    col_value = lax.all_to_all(value, "space", split_axis=2, concat_axis=1, tiled=True)
    col_maps = lax.all_to_all(maps, "space", split_axis=2, concat_axis=1, tiled=True)
    col_decay = lax.all_to_all(logdecay, "space", split_axis=2, concat_axis=1, tiled=True)
    column_out = scan_grid(col_value, col_maps, col_decay, False).astype(jnp.bfloat16)
    column_back = lax.all_to_all(column_out, "space", split_axis=1, concat_axis=2, tiled=True)
    row_out = scan_grid(value, maps, logdecay, True)
    skip_wide = jnp.repeat(skip, HEAD_DIM)
    total = row_out + column_back.astype(jnp.float32) + skip_wide * inner.astype(jnp.float32)
    group = NORM_HEADS * HEAD_DIM
    grouped = total.reshape(lead + (inner.shape[3] // group, group))
    norm_scale = lax.rsqrt(jnp.mean(grouped * grouped, axis=-1, keepdims=True) + EPS)
    gated = ((grouped * norm_scale).reshape(inner.shape) * norm_gain).astype(jnp.bfloat16)
    partial_out = jnp.einsum("irwc,cd->irwd", gated, w_out, preferred_element_type=jnp.float32)
    mixer = lax.psum_scatter(partial_out, "tensor", scatter_dimension=3, tiled=True)
    return (tokens + mixer).astype(jnp.bfloat16)


def solution(mesh):
    return jax.shard_map(
        on_device,
        mesh=mesh,
        in_specs=(
            P(None, "space", None, "tensor"),
            P(),
            P(None, "tensor"),
            P(),
            P(None, "tensor"),
            P("tensor"),
            P("tensor"),
            P("tensor"),
            P("tensor"),
            P("tensor", None),
        ),
        out_specs=P(None, "space", None, "tensor"),
        check_vma=False,
    )
```

profile of v0, /device:TPU:19, one launch (start us, length us, event | category | flops | bytes accessed | tf_op | source)
XLA Modules:
  0.0 218.5 jit_solution(5063790395113188788)
XLA Ops:
  6.6 1.9 convert_element_type.76
  8.5 0.7 neg.11
  9.2 45.6 %all-gather.2.cloned.1.call-done = bf16[2,2,128,2048]{3,2,1,0:T(8,128)(2,1)} async-done(((bf16[2,2,128,256]{3,2,1,0:T(8,128)(2,1)}), bf16[2,2,128,2048]{3,2,1,0:T(8,128)(2,1)}) %all-gather.2.cloned.1.call-update) | async-done | bytes 2097168 | tf_op jit(solution)/shard_map/all_gather | solution.py:52
  54.7 2.2 %fusion = f32[2,2,128]{2,1,0:T(2,128)S(1)} fusion(bf16[2,2,128,2048]{3,2,1,0:T(8,128)(2,1)} %all-gather.2.cloned.1.call-done), kind=kLoop, calls=%fused_computation.2 | loop fusion | flops 3145216 | bytes 2099200 | tf_op jit(solution)/shard_map/reduce_sum | solution.py:54
  57.0 0.8 multiply_convert_fusion.7
  57.8 0.8 copy.52
  58.6 12.8 %all-to-all-start.2 = ((bf16[2,2,128,6]{3,1,0,2:T(2,128)(2,1)}), bf16[2,2,128,6]{3,1,0,2:T(2,128)(2,1)S(1)}, u32[]{:S(2)}, u32[]{:S(2)}) async-start(bf16[2,2,128,6]{3,1,0,2:T(2,128)(2,1)} %copy.52), calls=%async_computation.2 | async-start | bytes 262144 | tf_op jit(solution)/shard_map/all_to_all | solution.py:75
  71.5 2.4 %convolution_convert_fusion.1 = bf16[2,2,128,256]{3,2,1,0:T(8,128)(2,1)S(1)} fusion(bf16[2,2,128,2048]{3,2,1,0:T(8,128)(2,1)} %all-gather.2.cloned.1.call-done, f32[2048]{0:T(1024)S(1)} %copy-done.13, f32[2,2,128]{2,1,0:T(2,128)S(1)} %add_rsqrt_fusion.1, bf16[2048,256]{1,0:T(8,128)(2,1)S(1)} %copy-done.11), kind=kOutput, calls=%fused_computation.14 | convolution fusion | flops 541196288 | bytes 3418112 | tf_op jit(solution)/shard_map/irwd,dc->irwc/dot_general | solution.py:59
  73.8 1.0 copy.48
  74.8 5.6 %all-to-all-done.2 = bf16[2,2,128,6]{3,1,0,2:T(2,128)(2,1)S(1)} async-done(((bf16[2,2,128,6]{3,1,0,2:T(2,128)(2,1)}), bf16[2,2,128,6]{3,1,0,2:T(2,128)(2,1)S(1)}, u32[]{:S(2)}, u32[]{:S(2)}) %all-to-all-start.2) | async-done | bytes 6176 | tf_op jit(solution)/shard_map/all_to_all | solution.py:75
  80.5 6.1 %all-to-all-start.1 = ((bf16[2,2,128,256]{3,1,0,2:T(2,128)(2,1)}), bf16[2,2,128,256]{3,1,0,2:T(2,128)(2,1)S(1)}, u32[]{:S(2)}, u32[]{:S(2)}) async-start(bf16[2,2,128,256]{3,1,0,2:T(2,128)(2,1)} %copy.48), calls=%async_computation.1 | async-start | bytes 524288 | tf_op jit(solution)/shard_map/all_to_all | solution.py:74
  86.6 0.7 mul.106
  87.4 1.2 copy.44
  88.5 4.4 %multiply_convert_fusion.5 = (bf16[2,2,128,384]{3,2,1,0:T(8,128)(2,1)S(1)}, f32[2,2,128,384]{3,2,1,0:T(8,128)}) fusion(f32[2,2,128,384]{3,2,1,0:T(8,128)} %copy.44, bf16[2048,384]{1,0:T(8,128)(2,1)} %param.12, bf16[2,2,128,2048]{3,2,1,0:T(8,128)(2,1)} %all-gather.2.cloned.1.call-done, f32[2048]{0:T(1024)S(1)} %copy-done.13, ...), kind=kOutput, calls=%fused_computation.34 | convolution fusion | flops 810287104 | bytes 5646336 | tf_op jit(solution)/shard_map/irwd,dc->irwc/dot_general | solution.py:56
  92.9 1.1 copy.46
  94.1 2.0 all-to-all-done.1
  96.1 8.8 %all-to-all-start = ((bf16[2,2,128,384]{3,1,0,2:T(2,128)(2,1)}), bf16[2,2,128,384]{3,1,0,2:T(2,128)(2,1)S(1)}, u32[]{:S(2)}, u32[]{:S(2)}) async-start(bf16[2,2,128,384]{3,1,0,2:T(2,128)(2,1)} %copy.46), calls=%async_computation | async-start | bytes 786432 | tf_op jit(solution)/shard_map/all_to_all | solution.py:73
  106.1 1.1 reduce_window_sum.18
  108.4 6.6 %all-to-all-done = bf16[2,2,128,384]{3,1,0,2:T(2,128)(2,1)S(1)} async-done(((bf16[2,2,128,384]{3,1,0,2:T(2,128)(2,1)}), bf16[2,2,128,384]{3,1,0,2:T(2,128)(2,1)S(1)}, u32[]{:S(2)}, u32[]{:S(2)}) %all-to-all-start) | async-done | bytes 393248 | tf_op jit(solution)/shard_map/all_to_all | solution.py:73
  115.3 1.6 reshape.67
  116.9 2.5 %convolution_convert_fusion = bf16[2,2,6,64,128]{4,3,2,1,0:T(8,128)(2,1)S(1)} fusion(bf16[2,128,2,6,64]{4,3,2,1,0:T(8,128)(2,1)} %reshape.67, f32[2,2,6,128]{3,2,1,0:T(8,128)} %bitcast_subtract_fusion, f32[2,2,6,128]{3,2,1,0:T(8,128)} %copy-done.3, f32[2,2,128,128]{3,2,1,0:T(8,128)S(1)} %fusion.40, pred[128,128]{1,0:T(8,128)(4,1)} %get-tuple-element.14, ...), kind=kOutput, calls=%fused_computation.13 | convolution fusion | flops 53280768 | bytes 1105920 | tf_op jit(solution)/shard_map/iahlm,imahp->ilahp/dot_general | solution.py:43
  119.4 1.1 copy.58
  120.5 10.5 %all-to-all-start.3 = ((bf16[2,128,2,384]{3,2,0,1:T(2,128)(2,1)}), bf16[2,128,2,384]{3,2,0,1:T(2,128)(2,1)S(1)}, u32[]{:S(2)}, u32[]{:S(2)}) async-start(bf16[2,128,2,384]{3,2,0,1:T(2,128)(2,1)} %copy.58), calls=%async_computation.3 | async-start | bytes 786432 | tf_op jit(solution)/shard_map/all_to_all | solution.py:77
  131.6 1.2 reduce_window_sum.17
  133.0 2.0 fusion.17
  135.1 1.4 copy.62
  136.5 4.8 %all-to-all-done.3 = bf16[2,128,2,384]{3,2,0,1:T(2,128)(2,1)S(1)} async-done(((bf16[2,128,2,384]{3,2,0,1:T(2,128)(2,1)}), bf16[2,128,2,384]{3,2,0,1:T(2,128)(2,1)S(1)}, u32[]{:S(2)}, u32[]{:S(2)}) %all-to-all-start.3) | async-done | bytes 393248 | tf_op jit(solution)/shard_map/all_to_all | solution.py:77
  142.2 1.4 reshape.68
  143.7 1.6 multiply_reduce_fusion
  145.3 3.3 %fusion.3 = f32[2,2,128,2048]{3,2,1,0:T(8,128)} fusion(bf16[384,2048]{1,0:T(8,128)(2,1)S(1)} %copy-done, f32[2,2,128,384]{3,2,1,0:T(8,128)S(1)} %get-tuple-element.6, f32[384]{0:T(512)S(1)} %copy-done.7, f32[2,2,128]{2,1,0:T(2,128)S(1)} %add_rsqrt_fusion), kind=kOutput, calls=%fused_computation.5 | convolution fusion | flops 805896192 | bytes 6557184 | tf_op jit(solution)/shard_map/irwc,cd->irwd/dot_general | solution.py:85
  148.6 61.3 %reduce-scatter.2.cloned.1.call-done = f32[2,2,128,256]{3,2,1,0:T(8,128)} async-done(((f32[2,2,128,2048]{3,2,1,0:T(8,128)}), f32[2,2,128,256]{3,2,1,0:T(8,128)}) %reduce-scatter.2.cloned.1.call-update) | async-done | bytes 524304 | tf_op jit(solution)/shard_map/reduce_scatter | solution.py:86
  209.8 1.8 add_convert_fusion
  (55 shorter events, 4.7 us)
Async XLA Ops:
  6.5 138.7 %copy-start = (bf16[384,2048]{1,0:T(8,128)(2,1)S(1)}, bf16[384,2048]{1,0:T(8,128)(2,1)}, u32[]{:S(2)}) copy-start(bf16[384,2048]{1,0:T(8,128)(2,1)} %param.19) | copy-start | bytes 4718596
  6.5 50.4 %copy-start.13 = (f32[2048]{0:T(1024)S(1)}, f32[2048]{0:T(1024)}, u32[]{:S(2)}) copy-start(f32[2048]{0:T(1024)} %param.11) | copy-start | bytes 24580
  6.5 50.4 %copy-start.14 = (f32[6]{0:T(128)S(1)}, f32[6]{0:T(128)}, u32[]{:S(2)}) copy-start(f32[6]{0:T(128)} %param.15) | copy-start | bytes 76
  6.5 50.5 %copy-start.12 = (bf16[2048,6]{0,1:T(8,128)(2,1)S(1)}, bf16[2048,6]{0,1:T(8,128)(2,1)}, u32[]{:S(2)}) copy-start(bf16[2048,6]{0,1:T(8,128)(2,1)} %param.14) | copy-start | bytes 73732
  6.5 48.2 %all-gather.2.cloned.1.call-start = ((), (), s32[]{:S(2)}) async-start(), calls=%async_computation.5 | async-start | bytes 2359296 | tf_op jit(solution)/shard_map/all_gather | solution.py:52
  9.2 48.7 %copy-start.8 = (f32[6]{0:T(128)}, f32[6]{0:T(128)S(1)}, u32[]{:S(2)}) copy-start(f32[6]{0:T(128)S(1)} %neg.11) | copy-start | bytes 76
  54.7 2.3 %copy-start.1 = (bf16[2,2,128,2048]{3,2,1,0:T(8,128)(2,1)S(1)}, bf16[2,2,128,2048]{3,2,1,0:T(8,128)(2,1)}, u32[]{:S(2)}) copy-start(bf16[2,2,128,2048]{3,2,1,0:T(8,128)(2,1)} %all-gather.2.cloned.1.call-done) | copy-start | bytes 6291460
  57.0 14.4 %copy-start.11 = (bf16[2048,256]{1,0:T(8,128)(2,1)S(1)}, bf16[2048,256]{1,0:T(8,128)(2,1)}, u32[]{:S(2)}) copy-start(bf16[2048,256]{1,0:T(8,128)(2,1)} %param.13) | copy-start | bytes 3145732
  58.6 21.8 %all-to-all-start.2 = ((bf16[2,2,128,6]{3,1,0,2:T(2,128)(2,1)}), bf16[2,2,128,6]{3,1,0,2:T(2,128)(2,1)S(1)}, u32[]{:S(2)}, u32[]{:S(2)}) async-start(bf16[2,2,128,6]{3,1,0,2:T(2,128)(2,1)} %copy.52), calls=%async_computation.2 | async-start | bytes 262144 | tf_op jit(solution)/shard_map/all_to_all | solution.py:75
  71.5 15.1 %copy-start.10 = (f32[6]{0:T(128)S(1)}, f32[6]{0:T(128)}, u32[]{:S(2)}) copy-start(f32[6]{0:T(128)} %param.17) | copy-start | bytes 76
  80.5 15.6 %all-to-all-start.1 = ((bf16[2,2,128,256]{3,1,0,2:T(2,128)(2,1)}), bf16[2,2,128,256]{3,1,0,2:T(2,128)(2,1)S(1)}, u32[]{:S(2)}, u32[]{:S(2)}) async-start(bf16[2,2,128,256]{3,1,0,2:T(2,128)(2,1)} %copy.48), calls=%async_computation.1 | async-start | bytes 524288 | tf_op jit(solution)/shard_map/all_to_all | solution.py:74
  96.1 18.9 %all-to-all-start = ((bf16[2,2,128,384]{3,1,0,2:T(2,128)(2,1)}), bf16[2,2,128,384]{3,1,0,2:T(2,128)(2,1)S(1)}, u32[]{:S(2)}, u32[]{:S(2)}) async-start(bf16[2,2,128,384]{3,1,0,2:T(2,128)(2,1)} %copy.46), calls=%async_computation | async-start | bytes 786432 | tf_op jit(solution)/shard_map/all_to_all | solution.py:73
  107.2 7.8 %copy-start.3 = (f32[2,2,6,128]{3,2,1,0:T(8,128)}, f32[2,2,6,128]{3,2,1,0:T(8,128)S(1)}, u32[]{:S(2)}) copy-start(f32[2,2,6,128]{3,2,1,0:T(8,128)S(1)} %reduce_window_sum.18) | copy-start | bytes 36868
  119.4 11.9 %copy-start.9 = (f32[6]{0:T(128)S(1)}, f32[6]{0:T(128)}, u32[]{:S(2)}) copy-start(f32[6]{0:T(128)} %copy-done.8) | copy-start | bytes 76
  119.4 13.6 %copy-start.4 = (pred[128,128]{1,0:T(8,128)(4,1)S(1)}, pred[128,128]{1,0:T(8,128)(4,1)}, u32[]{:S(2)}) copy-start(pred[128,128]{1,0:T(8,128)(4,1)} %get-tuple-element.14) | copy-start | bytes 49156
  119.4 13.6 %copy-start.5 = (pred[128,128]{1,0:T(8,128)(4,1)S(1)}, pred[128,128]{1,0:T(8,128)(4,1)}, u32[]{:S(2)}) copy-start(pred[128,128]{1,0:T(8,128)(4,1)} %get-tuple-element.15) | copy-start | bytes 49156
  120.5 20.8 %all-to-all-start.3 = ((bf16[2,128,2,384]{3,2,0,1:T(2,128)(2,1)}), bf16[2,128,2,384]{3,2,0,1:T(2,128)(2,1)S(1)}, u32[]{:S(2)}, u32[]{:S(2)}) async-start(bf16[2,128,2,384]{3,2,0,1:T(2,128)(2,1)} %copy.58), calls=%async_computation.3 | async-start | bytes 786432 | tf_op jit(solution)/shard_map/all_to_all | solution.py:77
  131.0 78.8 %reduce-scatter.2.cloned.1.call-start = ((), (), s32[]{:S(2)}) async-start(), calls=%async_computation.6 | async-start | bytes 4718592 | tf_op jit(solution)/shard_map/reduce_scatter | solution.py:86
  141.9 1.7 copy-start.6
  143.7 1.6 copy-start.7
  148.6 61.3 %copy-start.2 = (f32[2,2,128,256]{3,2,1,0:T(8,128)S(1)}, f32[2,2,128,256]{3,2,1,0:T(8,128)}, u32[]{:S(2)}) copy-start(f32[2,2,128,256]{3,2,1,0:T(8,128)} %param.10) | copy-start | bytes 1572868
Sparse Core Ops, SparseCore 0:
  9.5 45.2 all-gather.1
  148.7 61.0 reduce-scatter.1
where the time goes:
time: 219 us; the launch traced here: 218 us
  waiting for transfers between devices  126 us (58%)
  starting transfers between devices  38.4 us (18%)
  matrix products  15.8 us (7%)
  between operations  13.7 us (6%)
  local copies, waits for them, and re-layouts  12.8 us (6%)
  other arithmetic  11.9 us (5%)
    reduce_scatter x1, waiting for transfers between devices, on_device(): lax.psum_scatter(partial_out, 'tensor', scatter_dimension=3, tiled=True)  61.3 us
    all_gather x1, waiting for transfers between devices, on_device(): lax.all_gather(tokens.astype(jnp.bfloat16), 'tensor', axis=3, tiled=True)  45.6 us
    all_to_all x1, starting transfers between devices, on_device(): lax.all_to_all(logdecay, 'space', split_axis=2, concat_axis=1, tiled=True)  12.8 us
    all_to_all x1, starting transfers between devices, on_device(): lax.all_to_all(column_out, 'space', split_axis=1, concat_axis=2, tiled=True)  10.5 us
    all_to_all x1, starting transfers between devices, on_device(): lax.all_to_all(value, 'space', split_axis=2, concat_axis=1, tiled=True)  8.77 us
    all_to_all x1, waiting for transfers between devices, on_device(): lax.all_to_all(value, 'space', split_axis=2, concat_axis=1, tiled=True)  6.57 us
    all_to_all x1, starting transfers between devices, on_device(): lax.all_to_all(maps, 'space', split_axis=2, concat_axis=1, tiled=True)  6.09 us
    all_to_all x1, waiting for transfers between devices, on_device(): lax.all_to_all(logdecay, 'space', split_axis=2, concat_axis=1, tiled=True)  5.64 us
  transfers between devices with their start and end apart: 6, of which 6 were waited for; matrix products, arithmetic and copies ran while one was open for 9% of the time, Pallas kernels for 0%

commit v1 on v0

--- a/solution.py
+++ b/solution.py
@@ -7,6 +7,19 @@
 STATE = 128
 NORM_HEADS = 6
 EPS = 1e-05
+
+
+def map_field_over_axis(state):
+    latest = jnp.concatenate(
+        jax.lax.all_to_all(
+            jnp.stack(jax.lax.axis_size("tensor") * [state]),
+            concat_axis=0,
+            axis_name="tensor",
+            split_axis=0,
+        ),
+        axis=3,
+    )
+    return latest
 
 
 def kernel(logdecay):
@@ -49,7 +62,7 @@
 def on_device(
     tokens, in_gain, w_inner, w_bc, w_step, step_bias, decay_rate, skip, norm_gain, w_out
 ):
-    whole = lax.all_gather(tokens.astype(jnp.bfloat16), "tensor", axis=3, tiled=True)
+    whole = map_field_over_axis(tokens.astype(jnp.bfloat16))
     rounded = whole.astype(jnp.float32)
     scale = lax.rsqrt(jnp.mean(rounded * rounded, axis=-1, keepdims=True) + EPS)
     normed = (rounded * scale * in_gain).astype(jnp.bfloat16)

time: 219 us -> 235 us (1.073)
  starting transfers between devices: 38.4 us -> 45.1 us
  local copies, waits for them, and re-layouts: 12.8 us -> 18.6 us
  waiting for transfers between devices: 126 us -> 131 us
    all_to_all x0 -> x1, waiting for transfers between devices: none -> 49.1 us  [map_field_over_axis(): jax.lax.all_to_all(jnp.stack(jax.lax.axis_size('tensor') * [state]), conc...]
    all_gather x1 -> x0, waiting for transfers between devices: 45.6 us -> none  [on_device(): lax.all_gather(tokens.astype(jnp.bfloat16), 'tensor', axis=3, tiled=True)]
    all_to_all x0 -> x1, starting transfers between devices: none -> 7.85 us  [map_field_over_axis(): jax.lax.all_to_all(jnp.stack(jax.lax.axis_size('tensor') * [state]), conc...]
    all_to_all x0 -> x1, local copies, waits for them, and re-layouts: none -> 3.91 us  [map_field_over_axis(): jax.lax.all_to_all(jnp.stack(jax.lax.axis_size('tensor') * [state]), conc...]
  transfers between devices with their start and end apart: 6 -> 6, of which waited for: 6 -> 6; matrix products, arithmetic and copies ran while one was open for 9% -> 7% of each run, Pallas kernels for 0% -> 0%
where the time goes in v1:
time: 235 us; the launch traced here: 234 us
  waiting for transfers between devices  131 us (56%)
  starting transfers between devices  45.1 us (19%)
  local copies, waits for them, and re-layouts  18.6 us (8%)
  matrix products  14.9 us (6%)
  between operations  13.7 us (6%)
  other arithmetic  10.5 us (4%)
    reduce_scatter x1, waiting for transfers between devices, on_device(): lax.psum_scatter(partial_out, 'tensor', scatter_dimension=3, tiled=True)  61.4 us
    all_to_all x1, waiting for transfers between devices, map_field_over_axis(): jax.lax.all_to_all(jnp.stack(jax.lax.axis_size('tensor') * [state]), conc...  49.1 us
    all_to_all x1, starting transfers between devices, on_device(): lax.all_to_all(logdecay, 'space', split_axis=2, concat_axis=1, tiled=True)  13.3 us
    all_to_all x1, starting transfers between devices, on_device(): lax.all_to_all(column_out, 'space', split_axis=1, concat_axis=2, tiled=True)  10.1 us
    all_to_all x1, starting transfers between devices, on_device(): lax.all_to_all(value, 'space', split_axis=2, concat_axis=1, tiled=True)  7.85 us
    all_to_all x1, starting transfers between devices, map_field_over_axis(): jax.lax.all_to_all(jnp.stack(jax.lax.axis_size('tensor') * [state]), conc...  7.85 us
    all_to_all x1, waiting for transfers between devices, on_device(): lax.all_to_all(column_out, 'space', split_axis=1, concat_axis=2, tiled=True)  6.31 us
    all_to_all x1, waiting for transfers between devices, on_device(): lax.all_to_all(value, 'space', split_axis=2, concat_axis=1, tiled=True)  6.09 us
  transfers between devices with their start and end apart: 6, of which 6 were waited for; matrix products, arithmetic and copies ran while one was open for 7% of the time, Pallas kernels for 0%

profile of v1, /device:TPU:19, one launch (start us, length us, event | category | flops | bytes accessed | tf_op | source)
XLA Modules:
  0.0 234.2 jit_solution(297010515777903410)
XLA Ops:
  6.5 1.2 convert_element_type.86
  7.7 1.6 stack.2
  9.3 7.8 %all-to-all-start = ((bf16[8,2,2,128,256]{4,3,2,1,0:T(8,128)(2,1)}), bf16[8,2,2,128,256]{4,3,2,1,0:T(8,128)(2,1)}, u32[]{:S(2)}, u32[]{:S(2)}) async-start(bf16[8,2,2,128,256]{4,3,2,1,0:T(8,128)(2,1)} %stack.2), calls=%async_computation | async-start | bytes 4194304 | tf_op jit(solution)/shard_map/all_to_all | solution.py:14
  17.2 49.1 %all-to-all-done = bf16[8,2,2,128,256]{4,3,2,1,0:T(8,128)(2,1)} async-done(((bf16[8,2,2,128,256]{4,3,2,1,0:T(8,128)(2,1)}), bf16[8,2,2,128,256]{4,3,2,1,0:T(8,128)(2,1)}, u32[]{:S(2)}, u32[]{:S(2)}) %all-to-all-start) | async-done | bytes 2097184 | tf_op jit(solution)/shard_map/all_to_all | solution.py:14
  66.2 3.9 %copy.65 = bf16[8,2,2,128,256]{3,4,0,2,1:T(8,128)(2,1)} copy(bf16[8,2,2,128,256]{4,3,2,1,0:T(8,128)(2,1)} %all-to-all-done) | data formatting | bytes 4194304 | tf_op jit(solution)/shard_map/all_to_all | solution.py:14
  70.1 2.2 multiply_reduce_fusion
  73.0 1.3 copy-done.1
  74.7 0.8 copy.77
  75.6 13.3 %all-to-all-start.3 = ((bf16[2,2,128,6]{3,1,0,2:T(2,128)(2,1)}), bf16[2,2,128,6]{3,1,0,2:T(2,128)(2,1)S(1)}, u32[]{:S(2)}, u32[]{:S(2)}) async-start(bf16[2,2,128,6]{3,1,0,2:T(2,128)(2,1)} %copy.77), calls=%async_computation.3 | async-start | bytes 262144 | tf_op jit(solution)/shard_map/all_to_all | solution.py:88
  88.9 2.4 %convolution_convert_fusion.1 = bf16[2,2,128,256]{3,2,1,0:T(8,128)(2,1)S(1)} fusion(bf16[2,2,128,2048]{2,3,1,0:T(8,128)(2,1)} %copy-done.1, bf16[2048,256]{1,0:T(8,128)(2,1)S(1)} %copy-done.4), kind=kOutput, calls=%fused_computation.13 | convolution fusion | flops 537001984 | bytes 3407872 | tf_op jit(solution)/shard_map/irwd,dc->irwc/dot_general | solution.py:72
  91.3 1.0 copy.73
  92.2 5.6 %all-to-all-done.3 = bf16[2,2,128,6]{3,1,0,2:T(2,128)(2,1)S(1)} async-done(((bf16[2,2,128,6]{3,1,0,2:T(2,128)(2,1)}), bf16[2,2,128,6]{3,1,0,2:T(2,128)(2,1)S(1)}, u32[]{:S(2)}, u32[]{:S(2)}) %all-to-all-start.3) | async-done | bytes 6176 | tf_op jit(solution)/shard_map/all_to_all | solution.py:88
  97.8 6.0 %all-to-all-start.2 = ((bf16[2,2,128,256]{3,1,0,2:T(2,128)(2,1)}), bf16[2,2,128,256]{3,1,0,2:T(2,128)(2,1)}, u32[]{:S(2)}, u32[]{:S(2)}) async-start(bf16[2,2,128,256]{3,1,0,2:T(2,128)(2,1)} %copy.73), calls=%async_computation.2 | async-start | bytes 524288 | tf_op jit(solution)/shard_map/all_to_all | solution.py:87
  104.9 4.2 %multiply_convert_fusion.5 = (bf16[2,2,128,384]{3,2,1,0:T(8,128)(2,1)S(1)}, f32[2,2,128,384]{3,2,1,0:T(8,128)}) fusion(f32[2,2,128,384]{3,2,1,0:T(8,128)S(1)} %copy.68, bf16[2,2,128,2048]{2,3,1,0:T(8,128)(2,1)} %copy-done.1, bf16[2048,384]{1,0:T(8,128)(2,1)} %param.12), kind=kOutput, calls=%fused_computation.33 | convolution fusion | flops 806092800 | bytes 5636096 | tf_op jit(solution)/shard_map/irwd,dc->irwc/dot_general | solution.py:69
  109.1 1.1 copy.71
  110.3 3.0 %all-to-all-done.2 = bf16[2,2,128,256]{3,1,0,2:T(2,128)(2,1)} async-done(((bf16[2,2,128,256]{3,1,0,2:T(2,128)(2,1)}), bf16[2,2,128,256]{3,1,0,2:T(2,128)(2,1)}, u32[]{:S(2)}, u32[]{:S(2)}) %all-to-all-start.2) | async-done | bytes 262176 | tf_op jit(solution)/shard_map/all_to_all | solution.py:87
  113.3 7.8 %all-to-all-start.1 = ((bf16[2,2,128,384]{3,1,0,2:T(2,128)(2,1)}), bf16[2,2,128,384]{3,1,0,2:T(2,128)(2,1)S(1)}, u32[]{:S(2)}, u32[]{:S(2)}) async-start(bf16[2,2,128,384]{3,1,0,2:T(2,128)(2,1)} %copy.71), calls=%async_computation.1 | async-start | bytes 786432 | tf_op jit(solution)/shard_map/all_to_all | solution.py:86
  122.3 1.1 reduce_window_sum.18
  123.5 1.2 copy.74
  125.1 6.1 %all-to-all-done.1 = bf16[2,2,128,384]{3,1,0,2:T(2,128)(2,1)S(1)} async-done(((bf16[2,2,128,384]{3,1,0,2:T(2,128)(2,1)}), bf16[2,2,128,384]{3,1,0,2:T(2,128)(2,1)S(1)}, u32[]{:S(2)}, u32[]{:S(2)}) %all-to-all-start.1) | async-done | bytes 393248 | tf_op jit(solution)/shard_map/all_to_all | solution.py:86
  131.5 1.6 reshape.73
  133.0 2.5 %convolution_convert_fusion = bf16[2,2,6,64,128]{4,3,2,1,0:T(8,128)(2,1)S(1)} fusion(bf16[2,128,2,6,64]{4,3,2,1,0:T(8,128)(2,1)} %reshape.73, f32[2,2,6,128]{3,2,1,0:T(8,128)S(1)} %bitcast_subtract_fusion, f32[2,2,6,128]{3,2,1,0:T(8,128)S(1)} %reduce_window_sum.18, f32[2,2,128,128]{3,2,1,0:T(8,128)S(1)} %fusion.36, pred[128,128]{1,0:T(8,128)(4,1)S(1)} %copy-done.6, ...), kind=kOutput, calls=%fused_computation.12 | convolution fusion | flops 53280768 | bytes 1105920 | tf_op jit(solution)/shard_map/iahlm,imahp->ilahp/dot_general | solution.py:56
  135.5 1.1 copy.83
  136.6 10.1 %all-to-all-start.4 = ((bf16[2,128,2,384]{3,2,0,1:T(2,128)(2,1)}), bf16[2,128,2,384]{3,2,0,1:T(2,128)(2,1)S(1)}, u32[]{:S(2)}, u32[]{:S(2)}) async-start(bf16[2,128,2,384]{3,2,0,1:T(2,128)(2,1)} %copy.83), calls=%async_computation.4 | async-start | bytes 786432 | tf_op jit(solution)/shard_map/all_to_all | solution.py:90
  147.1 1.2 reduce_window_sum.17
  148.5 1.8 fusion.13
  150.6 6.3 %all-to-all-done.4 = bf16[2,128,2,384]{3,2,0,1:T(2,128)(2,1)S(1)} async-done(((bf16[2,128,2,384]{3,2,0,1:T(2,128)(2,1)}), bf16[2,128,2,384]{3,2,0,1:T(2,128)(2,1)S(1)}, u32[]{:S(2)}, u32[]{:S(2)}) %all-to-all-start.4) | async-done | bytes 393248 | tf_op jit(solution)/shard_map/all_to_all | solution.py:90
  157.8 1.4 reshape.75
  159.3 1.6 multiply_reduce_fusion.1
  160.9 3.3 %fusion.2 = f32[2,2,128,2048]{3,2,1,0:T(8,128)} fusion(bf16[384,2048]{1,0:T(8,128)(2,1)S(1)} %copy-done, f32[2,2,128,384]{3,2,1,0:T(8,128)S(1)} %get-tuple-element.6, f32[384]{0:T(512)S(1)} %copy-done.12, f32[2,2,128]{2,1,0:T(2,128)S(1)} %add_rsqrt_fusion), kind=kOutput, calls=%fused_computation.4 | convolution fusion | flops 805896192 | bytes 6557184 | tf_op jit(solution)/shard_map/irwc,cd->irwd/dot_general | solution.py:98
  164.2 61.4 %reduce-scatter.2.cloned.1.call-done = f32[2,2,128,256]{3,2,1,0:T(8,128)} async-done(((f32[2,2,128,2048]{3,2,1,0:T(8,128)}), f32[2,2,128,256]{3,2,1,0:T(8,128)}) %reduce-scatter.2.cloned.1.call-update) | async-done | bytes 524304 | tf_op jit(solution)/shard_map/reduce_scatter | solution.py:99
  225.6 1.8 add_convert_fusion
  (59 shorter events, 5.9 us)
Async XLA Ops:
  6.5 154.3 %copy-start = (bf16[384,2048]{1,0:T(8,128)(2,1)S(1)}, bf16[384,2048]{1,0:T(8,128)(2,1)}, u32[]{:S(2)}) copy-start(bf16[384,2048]{1,0:T(8,128)(2,1)} %param.19) | copy-start | bytes 4718596
  9.3 7.8 %copy-start.15 = (f32[6]{0:T(128)S(1)}, f32[6]{0:T(128)}, u32[]{:S(2)}) copy-start(f32[6]{0:T(128)} %param.16) | copy-start | bytes 76
  9.3 56.9 %all-to-all-start = ((bf16[8,2,2,128,256]{4,3,2,1,0:T(8,128)(2,1)}), bf16[8,2,2,128,256]{4,3,2,1,0:T(8,128)(2,1)}, u32[]{:S(2)}, u32[]{:S(2)}) async-start(bf16[8,2,2,128,256]{4,3,2,1,0:T(8,128)(2,1)} %stack.2), calls=%async_computation | async-start | bytes 4194304 | tf_op jit(solution)/shard_map/all_to_all | solution.py:14
  17.1 55.8 %copy-start.8 = (f32[6]{0:T(128)}, f32[6]{0:T(128)S(1)}, u32[]{:S(2)}) copy-start(f32[6]{0:T(128)S(1)} %neg.11) | copy-start | bytes 76
  66.2 6.1 %copy-start.10 = (f32[2048]{0:T(1024)S(1)}, f32[2048]{0:T(1024)}, u32[]{:S(2)}) copy-start(f32[2048]{0:T(1024)} %param.11) | copy-start | bytes 24580
  70.1 2.2 copy-start.2
  72.4 2.0 copy-start.5
  72.4 2.0 copy-start.13
  73.0 1.3 copy-start.1
  74.3 14.6 %copy-start.4 = (bf16[2048,256]{1,0:T(8,128)(2,1)S(1)}, bf16[2048,256]{1,0:T(8,128)(2,1)}, u32[]{:S(2)}) copy-start(bf16[2048,256]{1,0:T(8,128)(2,1)} %param.13) | copy-start | bytes 3145732
  75.6 22.3 %all-to-all-start.3 = ((bf16[2,2,128,6]{3,1,0,2:T(2,128)(2,1)}), bf16[2,2,128,6]{3,1,0,2:T(2,128)(2,1)S(1)}, u32[]{:S(2)}, u32[]{:S(2)}) async-start(bf16[2,2,128,6]{3,1,0,2:T(2,128)(2,1)} %copy.77), calls=%async_computation.3 | async-start | bytes 262144 | tf_op jit(solution)/shard_map/all_to_all | solution.py:88
  88.9 14.9 %copy-start.14 = (f32[6]{0:T(128)S(1)}, f32[6]{0:T(128)}, u32[]{:S(2)}) copy-start(f32[6]{0:T(128)} %param.17) | copy-start | bytes 76
  97.8 15.4 %all-to-all-start.2 = ((bf16[2,2,128,256]{3,1,0,2:T(2,128)(2,1)}), bf16[2,2,128,256]{3,1,0,2:T(2,128)(2,1)}, u32[]{:S(2)}, u32[]{:S(2)}) async-start(bf16[2,2,128,256]{3,1,0,2:T(2,128)(2,1)} %copy.73), calls=%async_computation.2 | async-start | bytes 524288 | tf_op jit(solution)/shard_map/all_to_all | solution.py:87
  113.3 17.9 %all-to-all-start.1 = ((bf16[2,2,128,384]{3,1,0,2:T(2,128)(2,1)}), bf16[2,2,128,384]{3,1,0,2:T(2,128)(2,1)S(1)}, u32[]{:S(2)}, u32[]{:S(2)}) async-start(bf16[2,2,128,384]{3,1,0,2:T(2,128)(2,1)} %copy.71), calls=%async_computation.1 | async-start | bytes 786432 | tf_op jit(solution)/shard_map/all_to_all | solution.py:86
  124.6 8.4 %copy-start.6 = (pred[128,128]{1,0:T(8,128)(4,1)S(1)}, pred[128,128]{1,0:T(8,128)(4,1)}, u32[]{:S(2)}) copy-start(pred[128,128]{1,0:T(8,128)(4,1)} %get-tuple-element.14) | copy-start | bytes 49156
  124.7 8.4 %copy-start.7 = (pred[128,128]{1,0:T(8,128)(4,1)S(1)}, pred[128,128]{1,0:T(8,128)(4,1)}, u32[]{:S(2)}) copy-start(pred[128,128]{1,0:T(8,128)(4,1)} %get-tuple-element.15) | copy-start | bytes 49156
  135.5 11.3 %copy-start.9 = (f32[6]{0:T(128)S(1)}, f32[6]{0:T(128)}, u32[]{:S(2)}) copy-start(f32[6]{0:T(128)} %copy-done.8) | copy-start | bytes 76
  136.6 20.3 %all-to-all-start.4 = ((bf16[2,128,2,384]{3,2,0,1:T(2,128)(2,1)}), bf16[2,128,2,384]{3,2,0,1:T(2,128)(2,1)S(1)}, u32[]{:S(2)}, u32[]{:S(2)}) async-start(bf16[2,128,2,384]{3,2,0,1:T(2,128)(2,1)} %copy.83), calls=%async_computation.4 | async-start | bytes 786432 | tf_op jit(solution)/shard_map/all_to_all | solution.py:90
  146.7 78.8 %reduce-scatter.2.cloned.1.call-start = ((), (), s32[]{:S(2)}) async-start(), calls=%async_computation.6 | async-start | bytes 4718592 | tf_op jit(solution)/shard_map/reduce_scatter | solution.py:99
  157.6 1.7 copy-start.11
  159.3 1.6 copy-start.12
  164.2 61.4 %copy-start.3 = (f32[2,2,128,256]{3,2,1,0:T(8,128)S(1)}, f32[2,2,128,256]{3,2,1,0:T(8,128)}, u32[]{:S(2)}) copy-start(f32[2,2,128,256]{3,2,1,0:T(8,128)} %param.10) | copy-start | bytes 1572868
Sparse Core Ops, SparseCore 0:
  164.3 61.2 reduce-scatter.1
